TPU v7x, 32 devices: a whole 2x2x4 slice. The times are simulated.
32 devices in a mesh: span: 2 (over y), height: 4 (over x, core), depth: 4 (over z).
Axes of the slice: x: 2, y: 2, z: 4, core: 2. Of those that a mesh axis runs over, the one named last changes fastest.
Arguments:
- load: float32 [8, 32, 64, 512], P(None, 'span', 'height', 'depth'), may hold values from -6 to 6
- phase: float32 [32, 64, 512], P('span', 'height', 'depth'), may hold values from 0.1 to 1
- void: int32 [4, 8, 64], P('span', 'height', 'depth'), may hold values from 0 to 1, as said below
- owner: int32 [4, 8, 64], P('span', 'height', 'depth'), may hold values from 0 to 1, as said below
- precond: bfloat16 [512, 512, 512], P(('span', 'height', 'depth')), may hold values from -1 to 2, as said below
Outputs:
- displacement: float32 [8, 32, 64, 512], P(None, 'span', 'height', 'depth')
- sensitivity: float32 [32, 64, 512], P('span', 'height', 'depth')
- phase_next: float32 [32, 64, 512], P('span', 'height', 'depth')
Inputs may be any that keep to these rules, and one draw needn't show every extreme that they name: `void`: each device's block of 16 x 16 x 128 cells holds at most 16 solid bricks; some device holds exactly 16. `owner`: among the solid bricks of one device at most 8 name any one value; on some device every value is named by exactly 8 solid bricks. Values of void bricks carry no meaning. `precond`: every block is symmetric with a positive diagonal that dominates each row.
All inputs are finite; a program needn't handle non-finite values.
Results may differ from a plain program's by a relative error of at most 0.0021.
Values may be sent and summed in bfloat16 or wider, within the bound.
No kernel may reach another device: no remote copies, remote signals or barrier semaphores. Data moves between devices by JAX's collectives and lax.ppermute only.
A program may use at most 128 MiB of HBM per device.

v0:
```python
import jax
import jax.numpy as jnp
from jax import lax
from jax.sharding import PartitionSpec as P

BE = 8
ITERS = 2
SWEEPS = 2
void_stiffness = 0.001
spring_rate = 0.05
time_step = 0.5
interface_weight = 0.5
epsilon_peak = 1e-06


def padded_2(block, sides, width):
    for axis, dim in sides:
        count = lax.axis_size(axis)
        forward = [(i, i + 1) for i in range(count - 1)]
        backward = [(target, source) for source, target in forward]
        low = lax.ppermute(
            lax.slice_in_dim(block, block.shape[dim] - width, None, axis=dim), axis, forward
        )
        high = lax.ppermute(lax.slice_in_dim(block, 0, width, axis=dim), axis, backward)
        block = jnp.concatenate([low, block, high], axis=dim)
    return block


def neighbours(padded):
    return [
        padded[..., 2:, 1:-1, 1:-1],
        padded[..., :-2, 1:-1, 1:-1],
        padded[..., 1:-1, 2:, 1:-1],
        padded[..., 1:-1, :-2, 1:-1],
        padded[..., 1:-1, 1:-1, 2:],
        padded[..., 1:-1, 1:-1, :-2],
    ]


def halo_stack(stacked):
    return padded_2(stacked, (("span", 1), ("height", 2), ("depth", 3)), 1)


def cell_sums(first, second):
    return jnp.sum(first * second, axis=(1, 2, 3))


def paired_sums(residual, search, image):
    return lax.psum(
        (cell_sums(residual, search), cell_sums(image, search)), ("span", "height", "depth")
    )


def local(load, phase, void, owner, precond):
    extents = phase.shape
    bricks_x, bricks_y, bricks_z = void.shape
    solid_bricks = (1 - void).astype(jnp.float32)
    expanded = jnp.broadcast_to(
        solid_bricks[:, None, :, None, :, None], (bricks_x, BE, bricks_y, BE, bricks_z, BE)
    )
    cell_mask = expanded.reshape(extents)
    stiffness = void_stiffness + (1.0 - void_stiffness) * phase**3
    coefficients = halo_stack(jnp.stack([cell_mask, cell_mask * stiffness]))
    near_pairs = neighbours(coefficients)
    weights = [cell_mask * 0.5 * (pair[0] * stiffness + pair[1]) for pair in near_pairs]

    def operate(field):
        padded = halo_stack(field)
        total = cell_mask * spring_rate * field
        for weight, near in zip(weights, neighbours(padded)):
            total = total + weight * (field - near)
        return (total, padded)

    span_count = lax.axis_size("span")
    slot_count = precond.shape[0]
    capacity = slot_count // span_count
    solid_flat = (1 - void).reshape(-1)
    owner_flat = owner.reshape(-1)
    columns = jnp.arange(span_count, dtype=jnp.int32)
    onehot = (owner_flat[:, None] == columns[None, :]).astype(jnp.int32) * solid_flat[:, None]
    before = jnp.cumsum(onehot, axis=0) - onehot
    rank = jnp.sum(before * onehot, axis=1)
    slot_of_brick = owner_flat * capacity + rank
    slot_ids = jnp.arange(slot_count, dtype=jnp.int32)
    matched = (slot_of_brick[None, :] == slot_ids[:, None]).astype(jnp.float32) * solid_flat[
        None, :
    ].astype(jnp.float32)
    selector = matched.reshape(slot_count, bricks_x, bricks_y, bricks_z)
    selector_low = selector.astype(jnp.bfloat16)
    loads = load.shape[0]

    def apply_blocks(incoming):
        image = jnp.einsum("sij,slj->sli", precond, incoming, preferred_element_type=jnp.float32)
        return lax.all_to_all(image, "span", split_axis=0, concat_axis=0, tiled=True)

    def precondition(residual):
        split = residual.astype(jnp.bfloat16).reshape(
            loads, bricks_x, BE, bricks_y, BE, bricks_z, BE
        )
        outgoing = jnp.einsum(
            "sxyz,lxiyjzk->slijk", selector_low, split, preferred_element_type=jnp.float32
        )
        outgoing = outgoing.astype(jnp.bfloat16).reshape(slot_count, loads, BE**3)
        returned = apply_blocks(
            lax.all_to_all(outgoing, "span", split_axis=0, concat_axis=0, tiled=True)
        )
        shaped = returned.reshape(slot_count, loads, BE, BE, BE)
        placed = jnp.einsum(
            "sxyz,slijk->lxiyjzk", selector, shaped, precision=lax.Precision.HIGHEST
        )
        return placed.reshape(loads, extents[0], extents[1], extents[2])

    right_side = cell_mask[None] * load
    solution = jnp.zeros_like(right_side)
    padded_solution = 0.0
    residual = right_side
    search = precondition(residual)
    image, padded_search = operate(search)
    norm_now, curvature_sum = paired_sums(residual, search, image)
    step_size = norm_now / curvature_sum
    direction = search
    padded_direction = padded_search
    along = image
    for iteration in range(ITERS):
        solution = solution + step_size[:, None, None, None] * direction
        padded_solution = padded_solution + step_size[:, None, None, None] * padded_direction
        residual = residual - step_size[:, None, None, None] * along
        if iteration + 1 < ITERS:
            search = precondition(residual)
            image, padded_search = operate(search)
            norm_next, curvature_sum = paired_sums(residual, search, image)
            factor = norm_next / norm_now
            step_size = norm_next / (curvature_sum - factor * norm_next / step_size)
            direction = search + factor[:, None, None, None] * direction
            padded_direction = padded_search + factor[:, None, None, None] * padded_direction
            along = image + factor[:, None, None, None] * along
            norm_now = norm_next
    solution_padded = halo_stack(solution)
    energy = jnp.zeros_like(phase)
    for pair, near in zip(near_pairs, neighbours(solution_padded)):
        energy = energy + pair[0] * jnp.sum((solution - near) ** 2, axis=0)
    sensitivity = -1.5 * (1.0 - void_stiffness) * phase**2 * cell_mask * energy
    peak_value = lax.pmax(jnp.max(-sensitivity), ("span", "height", "depth"))
    drive = (
        phase / time_step
        - 0.5 * phase * (1.0 - phase) * (1.0 - 2.0 * phase)
        - sensitivity / (peak_value + epsilon_peak)
    )
    inverse = 1.0 / (1.0 / time_step + 6.0 * interface_weight)
    current = phase
    for sweep_index in range(SWEEPS):
        padded = padded_2(
            current.astype(jnp.bfloat16), (("span", 0), ("height", 1), ("depth", 2)), 1
        ).astype(current.dtype)
        beside_all = neighbours(padded)
        current = (
            drive
            + interface_weight
            * (
                beside_all[0]
                + beside_all[1]
                + beside_all[2]
                + beside_all[3]
                + beside_all[4]
                + beside_all[5]
            )
        ) * inverse
    return (solution, sensitivity, current)


def solution(mesh):
    return jax.shard_map(
        local,
        mesh=mesh,
        in_specs=(
            P(None, "span", "height", "depth"),
            P("span", "height", "depth"),
            P("span", "height", "depth"),
            P("span", "height", "depth"),
            P(("span", "height", "depth"), None, None),
        ),
        out_specs=(
            P(None, "span", "height", "depth"),
            P("span", "height", "depth"),
            P("span", "height", "depth"),
        ),
        check_vma=False,
    )
```

profile of v0, /device:TPU:14, one launch (start us, length us, event | category | flops | bytes accessed | tf_op | source)
XLA Modules:
  0.0 461.7 jit_solution(4808410751461738423)
XLA Ops:
  10.2 10.6 %reshape.116 = bf16[8,2,8,2,8,16,8]{6,5,4,3,2,1,0:T(8,128)(2,1)} reshape(bf16[8,16,16,128]{3,2,1,0:T(8,128)(2,1)S(1)} %multiply_convert_fusion) | data formatting | bytes 1048576 | tf_op jit(solution)/shard_map/reshape | solution.py:97
  25.2 6.2 %bitcast_convert_fusion.1 = bf16[16,8,8,8,8]{0,4,3,2,1:T(8,128)(2,1)S(1)} fusion(bf16[8,2,8,2,8,16,8]{6,5,4,3,2,1,0:T(8,128)(2,1)} %reshape.116, f32[2,2,16]{2,1,0:T(2,128)S(1)} %copy-done.42, s32[2,2,16]{2,1,0:T(2,128)S(1)} %multiply_add_fusion.1), kind=kOutput, calls=%fused_computation.3 | convolution fusion | flops 8456192 | bytes 655872 | tf_op jit(solution)/shard_map/sxyz,lxiyjzk->slijk/dot_general | solution.py:100
  32.5 6.0 %all-to-all-start = ((bf16[16,8,512]{2,1,0:T(8,128)(2,1)}), bf16[16,8,512]{2,1,0:T(8,128)(2,1)S(1)}, u32[]{:S(2)}, u32[]{:S(2)}) async-start(bf16[16,8,512]{2,1,0:T(8,128)(2,1)} %copy.23), calls=%async_computation | async-start | bytes 262144 | tf_op jit(solution)/shard_map/all_to_all | solution.py:105
  46.3 6.4 %fusion.123 = f32[16,8,512]{2,1,0:T(8,128)} fusion(bf16[16,8,512]{2,1,0:T(8,128)(2,1)S(1)} %all-to-all-done, bf16[16,512,512]{2,1,0:T(8,128)(2,1)} %param.9), kind=kOutput, calls=%fused_computation.250 | convolution fusion | flops 67108864 | bytes 8781824 | tf_op jit(solution)/shard_map/sij,slj->sli/dot_general | solution.py:93
  52.7 4.6 all-to-all-start.1
  62.1 9.5 %convolution_bitcast_fusion.1 = f32[8,2,8,2,8,16,8]{5,6,3,1,4,2,0:T(8,128)} fusion(f32[16,8,8,8,8,1,1]{0,4,6,5,3,2,1:T(8,128)S(1)} %bitcast.148, f32[2,2,16]{2,1,0:T(2,128)} %copy-done.41, s32[2,2,16]{2,1,0:T(2,128)} %copy-done.44), kind=kOutput, calls=%fused_computation.1 | convolution fusion | flops 50333696 | bytes 1311232 | tf_op jit(solution)/shard_map/sxyz,slijk->lxiyjzk/dot_general | solution.py:108
  71.7 12.3 %copy.25 = f32[8,2,8,2,8,16,8]{6,5,4,3,2,1,0:T(8,128)} copy(f32[8,2,8,2,8,16,8]{5,6,3,1,4,2,0:T(8,128)} %convolution_bitcast_fusion.1) | data formatting | bytes 2097152 | tf_op jit(solution)/shard_map/sxyz,slijk->lxiyjzk/transpose | solution.py:108
  84.0 11.8 %reshape.119 = f32[8,16,16,128]{3,2,1,0:T(8,128)S(1)} reshape(f32[8,2,8,2,8,16,8]{6,5,4,3,2,1,0:T(8,128)} %copy.25) | data formatting | bytes 2097152 | tf_op jit(solution)/shard_map/reshape | solution.py:111
  98.0 4.5 collective-permute-start.1
  132.5 5.9 %multiply_reduce_fusion.1 = (f32[8]{0:T(128)}, f32[8]{0:T(128)}, f32[8,16,16,128]{3,2,1,0:T(8,128)S(1)}) fusion(f32[8,16,16,128]{3,2,1,0:T(8,128)S(1)} %reshape.119, f32[8,16,16,128]{3,2,1,0:T(8,128)S(1)} %copy-done.1, f32[16,16,128]{2,1,0:T(8,128)S(1)} %mul.300, f32[8,18,1,128]{3,2,1,0:T(1,128)} %copy-done.33, f32[8,18,16,128]{3,2,1,0:T(8,128)} %copy-done.7, ...), kind=kLoop, calls=%fused_computation.104 | loop fusion | flops 8912880 | bytes 5673280 | tf_op jit(solution)/shard_map/reduce_sum | solution.py:45
  138.4 42.6 %all-reduce.1 = (f32[8]{0:T(128)}, f32[8]{0:T(128)}) all-reduce(f32[8]{0:T(128)} %get-tuple-element.10, f32[8]{0:T(128)} %get-tuple-element.9), channel_id=1, replica_groups=mesh['span'=2,'height'=4,'depth'=4] {'span','height','depth'}, use_global_device_ids=true, to_apply=%region_3.4 | all-reduce | flops 16 | bytes 128 | tf_op jit(solution)/shard_map/psum | solution.py:49
  183.2 11.9 %reshape.121 = bf16[8,2,8,2,8,16,8]{6,5,4,3,2,1,0:T(8,128)(2,1)} reshape(bf16[8,16,16,128]{3,2,1,0:T(8,128)(2,1)} %fusion.87) | data formatting | bytes 1048576 | tf_op jit(solution)/shard_map/reshape | solution.py:97
  195.1 6.2 %bitcast_convert_fusion = bf16[16,8,8,8,8]{0,4,3,2,1:T(8,128)(2,1)S(1)} fusion(bf16[8,2,8,2,8,16,8]{6,5,4,3,2,1,0:T(8,128)(2,1)} %reshape.121, f32[2,2,16]{2,1,0:T(2,128)} %copy-done.41, s32[2,2,16]{2,1,0:T(2,128)} %copy-done.44), kind=kOutput, calls=%fused_computation.2 | convolution fusion | flops 8456192 | bytes 655872 | tf_op jit(solution)/shard_map/sxyz,lxiyjzk->slijk/dot_general | solution.py:100
  201.7 5.5 %all_to_all.20 = bf16[16,8,512]{2,1,0:T(8,128)(2,1)S(1)} all-to-all(bf16[16,8,512]{2,1,0:T(8,128)(2,1)S(1)} %copy.31), channel_id=1, replica_groups=mesh['span'=2,'height'=4,'depth'=4] {'span'}, dimensions={0} | all-to-all | bytes 262144 | tf_op jit(solution)/shard_map/all_to_all | solution.py:105
  207.3 5.6 %fusion.124 = f32[16,8,512]{2,1,0:T(8,128)S(1)} fusion(bf16[16,8,512]{2,1,0:T(8,128)(2,1)S(1)} %all_to_all.20, bf16[16,512,512]{2,1,0:T(8,128)(2,1)} %param.9), kind=kOutput, calls=%fused_computation.251 | convolution fusion | flops 67108864 | bytes 8781824 | tf_op jit(solution)/shard_map/sij,slj->sli/dot_general | solution.py:93
  212.9 7.7 %all_to_all.21 = f32[16,8,512]{2,1,0:T(8,128)S(1)} all-to-all(f32[16,8,512]{2,1,0:T(8,128)S(1)} %fusion.124), channel_id=1, replica_groups=mesh['span'=2,'height'=4,'depth'=4] {'span'}, dimensions={0} | all-to-all | bytes 524288 | tf_op jit(solution)/shard_map/all_to_all | solution.py:94
  222.5 10.1 %convolution_bitcast_fusion = f32[8,2,8,2,8,16,8]{5,6,3,1,4,2,0:T(8,128)} fusion(f32[16,8,8,8,8,1,1]{0,4,6,5,3,2,1:T(8,128)} %bitcast.147, f32[2,2,16]{2,1,0:T(2,128)S(1)} %copy-done.43, s32[2,2,16]{2,1,0:T(2,128)S(1)} %copy-done.45), kind=kOutput, calls=%fused_computation | convolution fusion | flops 50333696 | bytes 1311232 | tf_op jit(solution)/shard_map/sxyz,slijk->lxiyjzk/dot_general | solution.py:108
  232.6 12.3 %copy.33 = f32[8,2,8,2,8,16,8]{6,5,4,3,2,1,0:T(8,128)} copy(f32[8,2,8,2,8,16,8]{5,6,3,1,4,2,0:T(8,128)} %convolution_bitcast_fusion) | data formatting | bytes 2097152 | tf_op jit(solution)/shard_map/sxyz,slijk->lxiyjzk/transpose | solution.py:108
  244.9 11.9 %reshape.124 = f32[8,16,16,128]{3,2,1,0:T(8,128)S(1)} reshape(f32[8,2,8,2,8,16,8]{6,5,4,3,2,1,0:T(8,128)} %copy.33) | data formatting | bytes 2097152 | tf_op jit(solution)/shard_map/reshape | solution.py:111
  258.8 4.5 collective-permute-start.25
  264.7 4.8 %collective-permute-start.12 = (f32[8,1,16,128]{3,2,1,0:T(8,128)S(1)}, f32[8,1,16,128]{3,2,1,0:T(8,128)S(1)}, u32[]{:S(2)}, u32[]{:S(2)}) collective-permute-start(f32[8,1,16,128]{3,2,1,0:T(8,128)S(1)} %get-tuple-element.34), channel_id=1, source_target_pairs={{16,0},{17,1},{18,2},{19,3},{20,4},{21,5},{22,6},{23,7},{24,8},{25... | collective-permute-start | bytes 196616 | tf_op jit(solution)/shard_map/ppermute | solution.py:24
  304.9 5.0 %fusion.22 = f32[8]{0:T(128)S(1)} fusion(f32[8,16,16,128]{3,2,1,0:T(8,128)S(1)} %reshape.124, f32[8,18,18,1]{3,2,1,0:T(8,128)} %copy.37, f32[8,18,1,128]{3,2,1,0:T(1,128)S(1)} %collective-permute-done.14, f32[8,18,16,128]{3,2,1,0:T(8,128)} %copy-done.8, f32[8,18,1,128]{3,2,1,0:T(1,128)} %copy-done.35, f32[8,18,18,1]{3,2,1,0:T(8,128)} %copy.35, ...), kind=kLoop, calls=%fused_computation.48 | loop fusion | flops 8126456 | bytes 3445024 | tf_op jit(solution)/shard_map/reduce_sum | solution.py:45
  310.0 39.8 %all-reduce = (f32[8]{0:T(128)S(1)}, f32[8]{0:T(128)S(1)}) all-reduce(f32[8]{0:T(128)S(1)} %copy-done.59, f32[8]{0:T(128)S(1)} %fusion.22), channel_id=1, replica_groups=mesh['span'=2,'height'=4,'depth'=4] {'span','height','depth'}, use_global_device_ids=true, to_apply=%region_7.8 | all-reduce | flops 16 | bytes 128 | tf_op jit(solution)/shard_map/psum | solution.py:49
  393.5 41.7 %pmax.7 = f32[]{:T(128)} all-reduce(f32[]{:T(128)} %get-tuple-element.15), channel_id=1, replica_groups=mesh['span'=2,'height'=4,'depth'=4] {'span','height','depth'}, use_global_device_ids=true, to_apply=%region_17.18 | all-reduce | flops 1 | bytes 8 | tf_op jit(solution)/shard_map/pmax | solution.py:143
  (269 shorter events, 171.4 us)
Async XLA Ops:
  5.8 15.1 %collective-permute-start = (f32[2,1,16,128]{3,2,1,0:T(8,128)S(1)}, f32[2,1,16,128]{3,2,1,0:T(8,128)S(1)}, u32[]{:S(2)}, u32[]{:S(2)}) collective-permute-start(f32[2,1,16,128]{3,2,1,0:T(8,128)S(1)} %get-tuple-element.49), channel_id=1, source_target_pairs={{16,0},{17,1},{18,2},{19,3},{20,4},{21,5},{22,6},{23,7},{24,8},{25... | collective-permute-start | bytes 49160 | tf_op jit(solution)/shard_map/ppermute | solution.py:24
  8.2 12.6 %collective-permute-start.2 = (f32[2,1,16,128]{3,2,1,0:T(8,128)S(1)}, f32[2,1,16,128]{3,2,1,0:T(8,128)S(1)}, u32[]{:S(2)}, u32[]{:S(2)}) collective-permute-start(f32[2,1,16,128]{3,2,1,0:T(8,128)S(1)} %get-tuple-element.48), channel_id=1, source_target_pairs={{0,16},{1,17},{2,18},{3,19},{4,20},{5,21},{6,22},{7,23},{8,24},{9,... | collective-permute-start | bytes 49160 | tf_op jit(solution)/shard_map/ppermute | solution.py:21
  20.9 17.6 %collective-permute-start.4 = (f32[2,18,1,128]{3,2,1,0:T(1,128)S(1)}, f32[2,18,1,128]{3,2,1,0:T(1,128)S(1)}, u32[]{:S(2)}, u32[]{:S(2)}) collective-permute-start(f32[2,18,1,128]{3,2,1,0:T(1,128)S(1)} %get-tuple-element.47), channel_id=1, source_target_pairs={{4,0},{8,4},{12,8},{5,1},{9,5},{13,9},{6,2},{10,6},{14,10},{7,3},{... | collective-permute-start | bytes 55304 | tf_op jit(solution)/shard_map/ppermute | solution.py:24
  22.8 15.7 %collective-permute-start.6 = (f32[2,18,1,128]{3,2,1,0:T(1,128)S(1)}, f32[2,18,1,128]{3,2,1,0:T(1,128)S(1)}, u32[]{:S(2)}, u32[]{:S(2)}) collective-permute-start(f32[2,18,1,128]{3,2,1,0:T(1,128)S(1)} %get-tuple-element.46), channel_id=1, source_target_pairs={{0,4},{4,8},{8,12},{1,5},{5,9},{9,13},{2,6},{6,10},{10,14},{3,7},{... | collective-permute-start | bytes 55304 | tf_op jit(solution)/shard_map/ppermute | solution.py:21
  32.5 13.9 %all-to-all-start = ((bf16[16,8,512]{2,1,0:T(8,128)(2,1)}), bf16[16,8,512]{2,1,0:T(8,128)(2,1)S(1)}, u32[]{:S(2)}, u32[]{:S(2)}) async-start(bf16[16,8,512]{2,1,0:T(8,128)(2,1)} %copy.23), calls=%async_computation | async-start | bytes 262144 | tf_op jit(solution)/shard_map/all_to_all | solution.py:105
  39.6 69.8 %collective-permute-start.10 = (f32[2,18,18,1]{3,2,1,0:T(8,128)}, f32[2,18,18,1]{3,2,1,0:T(8,128)}, u32[]{:S(2)}, u32[]{:S(2)}) collective-permute-start(f32[2,18,18,1]{3,2,1,0:T(8,128)} %get-tuple-element.45), channel_id=1, source_target_pairs={{0,1},{1,2},{2,3},{4,5},{5,6},{6,7},{8,9},{9,10},{10,11},{12,13},{... | collective-permute-start | bytes 7784 | tf_op jit(solution)/shard_map/ppermute | solution.py:21
  43.1 83.1 %collective-permute-start.8 = (f32[2,18,18,1]{3,2,1,0:T(8,128)}, f32[2,18,18,1]{3,2,1,0:T(8,128)}, u32[]{:S(2)}, u32[]{:S(2)}) collective-permute-start(f32[2,18,18,1]{3,2,1,0:T(8,128)} %get-tuple-element.44), channel_id=1, source_target_pairs={{1,0},{2,1},{3,2},{5,4},{6,5},{7,6},{9,8},{10,9},{11,10},{13,12},{... | collective-permute-start | bytes 7784 | tf_op jit(solution)/shard_map/ppermute | solution.py:24
  52.7 7.9 %all-to-all-start.1 = ((f32[16,8,512]{2,1,0:T(8,128)}), f32[16,8,512]{2,1,0:T(8,128)}, u32[]{:S(2)}, u32[]{:S(2)}) async-start(f32[16,8,512]{2,1,0:T(8,128)} %fusion.123), calls=%async_computation.1 | async-start | bytes 524288 | tf_op jit(solution)/shard_map/all_to_all | solution.py:94
  117.9 10.2 %collective-permute-start.11 = (f32[8,18,18,1]{2,0,3,1:T(8,128)S(1)}, f32[8,18,18,1]{2,0,3,1:T(8,128)S(1)}, u32[]{:S(2)}, u32[]{:S(2)}) collective-permute-start(f32[8,18,18,1]{2,0,3,1:T(8,128)S(1)} %copy.28), channel_id=1, source_target_pairs={{0,1},{1,2},{2,3},{4,5},{5,6},{6,7},{8,9},{9,10},{10,11},{12,13},{... | collective-permute-start | bytes 31112 | tf_op jit(solution)/shard_map/ppermute | solution.py:21
  123.1 7.2 %collective-permute-start.9 = (f32[8,18,18,1]{2,0,3,1:T(8,128)S(1)}, f32[8,18,18,1]{2,0,3,1:T(8,128)S(1)}, u32[]{:S(2)}, u32[]{:S(2)}) collective-permute-start(f32[8,18,18,1]{2,0,3,1:T(8,128)S(1)} %copy.26), channel_id=1, source_target_pairs={{1,0},{2,1},{3,2},{5,4},{6,5},{7,6},{9,8},{10,9},{11,10},{13,12},{... | collective-permute-start | bytes 31112 | tf_op jit(solution)/shard_map/ppermute | solution.py:24
  256.8 12.6 %collective-permute-start.13 = (f32[8,1,16,128]{3,2,1,0:T(8,128)S(1)}, f32[8,1,16,128]{3,2,1,0:T(8,128)S(1)}, u32[]{:S(2)}, u32[]{:S(2)}) collective-permute-start(f32[8,1,16,128]{3,2,1,0:T(8,128)S(1)} %get-tuple-element.35), channel_id=1, source_target_pairs={{0,16},{1,17},{2,18},{3,19},{4,20},{5,21},{6,22},{7,23},{8,24},{9,... | collective-permute-start | bytes 196616 | tf_op jit(solution)/shard_map/ppermute | solution.py:21
  258.8 17.9 %collective-permute-start.25 = (bf16[1,16,128]{2,1,0:T(8,128)(2,1)S(1)}, bf16[1,16,128]{2,1,0:T(8,128)(2,1)S(1)}, u32[]{:S(2)}, u32[]{:S(2)}) collective-permute-start(bf16[1,16,128]{2,1,0:T(8,128)(2,1)S(1)} %get-tuple-element.63), channel_id=1, source_target_pairs={{16,0},{17,1},{18,2},{19,3},{20,4},{21,5},{22,6},{23,7},{24,8},{25... | collective-permute-start | bytes 12296 | tf_op jit(solution)/shard_map/ppermute | solution.py:24
  263.4 13.4 %collective-permute-start.24 = (bf16[1,16,128]{2,1,0:T(8,128)(2,1)S(1)}, bf16[1,16,128]{2,1,0:T(8,128)(2,1)S(1)}, u32[]{:S(2)}, u32[]{:S(2)}) collective-permute-start(bf16[1,16,128]{2,1,0:T(8,128)(2,1)S(1)} %get-tuple-element.62), channel_id=1, source_target_pairs={{0,16},{1,17},{2,18},{3,19},{4,20},{5,21},{6,22},{7,23},{8,24},{9,... | collective-permute-start | bytes 12296 | tf_op jit(solution)/shard_map/ppermute | solution.py:21
  264.7 7.6 %collective-permute-start.12 = (f32[8,1,16,128]{3,2,1,0:T(8,128)S(1)}, f32[8,1,16,128]{3,2,1,0:T(8,128)S(1)}, u32[]{:S(2)}, u32[]{:S(2)}) collective-permute-start(f32[8,1,16,128]{3,2,1,0:T(8,128)S(1)} %get-tuple-element.34), channel_id=1, source_target_pairs={{16,0},{17,1},{18,2},{19,3},{20,4},{21,5},{22,6},{23,7},{24,8},{25... | collective-permute-start | bytes 196616 | tf_op jit(solution)/shard_map/ppermute | solution.py:24
  272.4 9.5 %collective-permute-start.14 = (f32[8,18,1,128]{3,2,1,0:T(1,128)S(1)}, f32[8,18,1,128]{3,2,1,0:T(1,128)S(1)}, u32[]{:S(2)}, u32[]{:S(2)}) collective-permute-start(f32[8,18,1,128]{3,2,1,0:T(1,128)S(1)} %get-tuple-element.29), channel_id=1, source_target_pairs={{4,0},{8,4},{12,8},{5,1},{9,5},{13,9},{6,2},{10,6},{14,10},{7,3},{... | collective-permute-start | bytes 221192 | tf_op jit(solution)/shard_map/ppermute | solution.py:24
  274.3 7.6 %collective-permute-start.15 = (f32[8,18,1,128]{3,2,1,0:T(1,128)S(1)}, f32[8,18,1,128]{3,2,1,0:T(1,128)S(1)}, u32[]{:S(2)}, u32[]{:S(2)}) collective-permute-start(f32[8,18,1,128]{3,2,1,0:T(1,128)S(1)} %get-tuple-element.28), channel_id=1, source_target_pairs={{0,4},{4,8},{8,12},{1,5},{5,9},{9,13},{2,6},{6,10},{10,14},{3,7},{... | collective-permute-start | bytes 221192 | tf_op jit(solution)/shard_map/ppermute | solution.py:21
  276.8 21.0 %collective-permute-start.27 = (bf16[18,1,128]{2,1,0:T(2,128)(2,1)S(1)}, bf16[18,1,128]{2,1,0:T(2,128)(2,1)S(1)}, u32[]{:S(2)}, u32[]{:S(2)}) collective-permute-start(bf16[18,1,128]{2,1,0:T(2,128)(2,1)S(1)} %get-tuple-element.59), channel_id=1, source_target_pairs={{4,0},{8,4},{12,8},{5,1},{9,5},{13,9},{6,2},{10,6},{14,10},{7,3},{... | collective-permute-start | bytes 13832 | tf_op jit(solution)/shard_map/ppermute | solution.py:24
  280.0 17.9 %collective-permute-start.26 = (bf16[18,1,128]{2,1,0:T(2,128)(2,1)S(1)}, bf16[18,1,128]{2,1,0:T(2,128)(2,1)S(1)}, u32[]{:S(2)}, u32[]{:S(2)}) collective-permute-start(bf16[18,1,128]{2,1,0:T(2,128)(2,1)S(1)} %get-tuple-element.58), channel_id=1, source_target_pairs={{0,4},{4,8},{8,12},{1,5},{5,9},{9,13},{2,6},{6,10},{10,14},{3,7},{... | collective-permute-start | bytes 13832 | tf_op jit(solution)/shard_map/ppermute | solution.py:21
  288.3 10.3 %collective-permute-start.17 = (f32[8,18,18,1]{2,0,3,1:T(8,128)}, f32[8,18,18,1]{2,0,3,1:T(8,128)}, u32[]{:S(2)}, u32[]{:S(2)}) collective-permute-start(f32[8,18,18,1]{2,0,3,1:T(8,128)} %copy.36), channel_id=1, source_target_pairs={{0,1},{1,2},{2,3},{4,5},{5,6},{6,7},{8,9},{9,10},{10,11},{12,13},{... | collective-permute-start | bytes 31112 | tf_op jit(solution)/shard_map/ppermute | solution.py:21
  294.6 7.1 %collective-permute-start.16 = (f32[8,18,18,1]{2,0,3,1:T(8,128)}, f32[8,18,18,1]{2,0,3,1:T(8,128)}, u32[]{:S(2)}, u32[]{:S(2)}) collective-permute-start(f32[8,18,18,1]{2,0,3,1:T(8,128)} %copy.34), channel_id=1, source_target_pairs={{1,0},{2,1},{3,2},{5,4},{6,5},{7,6},{9,8},{10,9},{11,10},{13,12},{... | collective-permute-start | bytes 31112 | tf_op jit(solution)/shard_map/ppermute | solution.py:24
  350.8 11.1 %collective-permute-start.18 = (f32[8,1,16,128]{3,2,1,0:T(8,128)S(1)}, f32[8,1,16,128]{3,2,1,0:T(8,128)S(1)}, u32[]{:S(2)}, u32[]{:S(2)}) collective-permute-start(f32[8,1,16,128]{3,2,1,0:T(8,128)S(1)} %get-tuple-element.33), channel_id=1, source_target_pairs={{16,0},{17,1},{18,2},{19,3},{20,4},{21,5},{22,6},{23,7},{24,8},{25... | collective-permute-start | bytes 196616 | tf_op jit(solution)/shard_map/ppermute | solution.py:24
  353.7 8.2 %collective-permute-start.19 = (f32[8,1,16,128]{3,2,1,0:T(8,128)S(1)}, f32[8,1,16,128]{3,2,1,0:T(8,128)S(1)}, u32[]{:S(2)}, u32[]{:S(2)}) collective-permute-start(f32[8,1,16,128]{3,2,1,0:T(8,128)S(1)} %get-tuple-element.32), channel_id=1, source_target_pairs={{0,16},{1,17},{2,18},{3,19},{4,20},{5,21},{6,22},{7,23},{8,24},{9,... | collective-permute-start | bytes 196616 | tf_op jit(solution)/shard_map/ppermute | solution.py:21
  356.1 10.3 %collective-permute-start.29 = (bf16[18,18,1]{2,1,0:T(8,128)(2,1)S(1)}, bf16[18,18,1]{2,1,0:T(8,128)(2,1)S(1)}, u32[]{:S(2)}, u32[]{:S(2)}) collective-permute-start(bf16[18,18,1]{2,1,0:T(8,128)(2,1)S(1)} %get-tuple-element.55), channel_id=1, source_target_pairs={{1,0},{2,1},{3,2},{5,4},{6,5},{7,6},{9,8},{10,9},{11,10},{13,12},{... | collective-permute-start | bytes 1952 | tf_op jit(solution)/shard_map/ppermute | solution.py:24
  374.7 8.4 %collective-permute-start.22 = (f32[8,18,18,1]{2,0,3,1:T(8,128)}, f32[8,18,18,1]{2,0,3,1:T(8,128)}, u32[]{:S(2)}, u32[]{:S(2)}) collective-permute-start(f32[8,18,18,1]{2,0,3,1:T(8,128)} %copy.38), channel_id=1, source_target_pairs={{1,0},{2,1},{3,2},{5,4},{6,5},{7,6},{9,8},{10,9},{11,10},{13,12},{... | collective-permute-start | bytes 31112 | tf_op jit(solution)/shard_map/ppermute | solution.py:24
  (76 other events, 874.3 us)
where the time goes:
time: 471 us; the launch traced here: 462 us
  blocking collectives  137 us (29%)
  local copies, waits for them, and re-layouts  121 us (26%)
  starting transfers between devices  102 us (22%)
  matrix products  44 us (9%)
  other arithmetic  34.2 us (7%)
  waiting for transfers between devices  19.7 us (4%)
    psum x2, blocking collectives, paired_sums(): lax.psum((cell_sums(residual, search), cell_sums(image, search)), ('span'...  82.4 us
    ppermute x18, starting transfers between devices, padded_2(): lax.ppermute(lax.slice_in_dim(block, 0, width, axis=dim), axis, backward)  53.1 us
    pmax x1, blocking collectives, local(): peak_value = lax.pmax(jnp.max(-sensitivity), ('span', 'height', 'depth'))  41.7 us
    ppermute x18, starting transfers between devices, padded_2(): lax.ppermute(lax.slice_in_dim(block, block.shape[dim] - width, None, axis...  38.7 us
    transpose x2, local copies, waits for them, and re-layouts, precondition(): jnp.einsum('sxyz,slijk->lxiyjzk', selector, shaped, precision=lax.Precisi...  24.7 us
    reshape x2, local copies, waits for them, and re-layouts, precondition(): return placed.reshape(loads, extents[0], extents[1], extents[2])  23.7 us
    reshape x2, local copies, waits for them, and re-layouts, precondition(): residual.astype(jnp.bfloat16)  22.5 us
    dot_general x2, matrix products, precondition(): jnp.einsum('sxyz,slijk->lxiyjzk', selector, shaped, precision=lax.Precisi...  19.6 us
  transfers between devices with their start and end apart: 38, of which 9 were waited for; matrix products, arithmetic and copies ran while one was open for 21% of the time, Pallas kernels for 0%

commit v1 on v0

--- a/solution.py
+++ b/solution.py
@@ -47,7 +47,8 @@
 
 def paired_sums(residual, search, image):
     return lax.psum(
-        (cell_sums(residual, search), cell_sums(image, search)), ("span", "height", "depth")
+        lax.psum((cell_sums(residual, search), cell_sums(image, search)), ("height", "depth")),
+        "span",
     )
 
 

time: 471 us -> 463 us (0.983)
  blocking collectives: 137 us -> 128 us
    psum x2 -> x4, blocking collectives: 82.4 us -> 72.3 us  [the longest x2 61.3 us: paired_sums(): lax.psum((cell_sums(residual, search), cell_sums(image, search)), ('heigh...]
  transfers between devices with their start and end apart: 38 -> 38, of which waited for: 9 -> 9; matrix products, arithmetic and copies ran while one was open for 21% -> 22% of each run, Pallas kernels for 0% -> 0%
where the time goes in v1:
time: 463 us; the launch traced here: 454 us
  blocking collectives  128 us (28%)
  local copies, waits for them, and re-layouts  121 us (26%)
  starting transfers between devices  103 us (22%)
  matrix products  44 us (10%)
  other arithmetic  34.2 us (7%)
  waiting for transfers between devices  20.1 us (4%)
    psum x2, blocking collectives, paired_sums(): lax.psum((cell_sums(residual, search), cell_sums(image, search)), ('heigh...  61.3 us
    ppermute x18, starting transfers between devices, padded_2(): lax.ppermute(lax.slice_in_dim(block, 0, width, axis=dim), axis, backward)  54.7 us
    pmax x1, blocking collectives, local(): peak_value = lax.pmax(jnp.max(-sensitivity), ('span', 'height', 'depth'))  41.3 us
    ppermute x18, starting transfers between devices, padded_2(): lax.ppermute(lax.slice_in_dim(block, block.shape[dim] - width, None, axis...  37.7 us
    transpose x2, local copies, waits for them, and re-layouts, precondition(): jnp.einsum('sxyz,slijk->lxiyjzk', selector, shaped, precision=lax.Precisi...  24.7 us
    reshape x2, local copies, waits for them, and re-layouts, precondition(): return placed.reshape(loads, extents[0], extents[1], extents[2])  23.7 us
    reshape x2, local copies, waits for them, and re-layouts, precondition(): residual.astype(jnp.bfloat16)  22.5 us
    dot_general x2, matrix products, precondition(): jnp.einsum('sxyz,slijk->lxiyjzk', selector, shaped, precision=lax.Precisi...  19.6 us
  transfers between devices with their start and end apart: 38, of which 9 were waited for; matrix products, arithmetic and copies ran while one was open for 22% of the time, Pallas kernels for 0%

profile of v1, /device:TPU:14, one launch (start us, length us, event | category | flops | bytes accessed | tf_op | source)
XLA Modules:
  0.0 453.5 jit_solution(16156356507478658724)
XLA Ops:
  10.2 10.6 %reshape.116 = bf16[8,2,8,2,8,16,8]{6,5,4,3,2,1,0:T(8,128)(2,1)} reshape(bf16[8,16,16,128]{3,2,1,0:T(8,128)(2,1)S(1)} %multiply_convert_fusion) | data formatting | bytes 1048576 | tf_op jit(solution)/shard_map/reshape | solution.py:98
  25.2 6.2 %bitcast_convert_fusion.1 = bf16[16,8,8,8,8]{0,4,3,2,1:T(8,128)(2,1)S(1)} fusion(bf16[8,2,8,2,8,16,8]{6,5,4,3,2,1,0:T(8,128)(2,1)} %reshape.116, f32[2,2,16]{2,1,0:T(2,128)S(1)} %copy-done.42, s32[2,2,16]{2,1,0:T(2,128)S(1)} %multiply_add_fusion.1), kind=kOutput, calls=%fused_computation.3 | convolution fusion | flops 8456192 | bytes 655872 | tf_op jit(solution)/shard_map/sxyz,lxiyjzk->slijk/dot_general | solution.py:101
  32.5 6.0 %all-to-all-start = ((bf16[16,8,512]{2,1,0:T(8,128)(2,1)}), bf16[16,8,512]{2,1,0:T(8,128)(2,1)S(1)}, u32[]{:S(2)}, u32[]{:S(2)}) async-start(bf16[16,8,512]{2,1,0:T(8,128)(2,1)} %copy.23), calls=%async_computation | async-start | bytes 262144 | tf_op jit(solution)/shard_map/all_to_all | solution.py:106
  46.4 6.4 %fusion.123 = f32[16,8,512]{2,1,0:T(8,128)} fusion(bf16[16,8,512]{2,1,0:T(8,128)(2,1)S(1)} %all-to-all-done, bf16[16,512,512]{2,1,0:T(8,128)(2,1)} %param.9), kind=kOutput, calls=%fused_computation.250 | convolution fusion | flops 67108864 | bytes 8781824 | tf_op jit(solution)/shard_map/sij,slj->sli/dot_general | solution.py:94
  52.7 4.6 %all-to-all-start.1 = ((f32[16,8,512]{2,1,0:T(8,128)}), f32[16,8,512]{2,1,0:T(8,128)}, u32[]{:S(2)}, u32[]{:S(2)}) async-start(f32[16,8,512]{2,1,0:T(8,128)} %fusion.123), calls=%async_computation.1 | async-start | bytes 524288 | tf_op jit(solution)/shard_map/all_to_all | solution.py:95
  62.2 9.5 %convolution_bitcast_fusion.1 = f32[8,2,8,2,8,16,8]{5,6,3,1,4,2,0:T(8,128)} fusion(f32[16,8,8,8,8,1,1]{0,4,6,5,3,2,1:T(8,128)S(1)} %bitcast.148, f32[2,2,16]{2,1,0:T(2,128)} %copy-done.41, s32[2,2,16]{2,1,0:T(2,128)} %copy-done.44), kind=kOutput, calls=%fused_computation.1 | convolution fusion | flops 50333696 | bytes 1311232 | tf_op jit(solution)/shard_map/sxyz,slijk->lxiyjzk/dot_general | solution.py:109
  71.7 12.3 %copy.25 = f32[8,2,8,2,8,16,8]{6,5,4,3,2,1,0:T(8,128)} copy(f32[8,2,8,2,8,16,8]{5,6,3,1,4,2,0:T(8,128)} %convolution_bitcast_fusion.1) | data formatting | bytes 2097152 | tf_op jit(solution)/shard_map/sxyz,slijk->lxiyjzk/transpose | solution.py:109
  84.0 11.8 %reshape.119 = f32[8,16,16,128]{3,2,1,0:T(8,128)S(1)} reshape(f32[8,2,8,2,8,16,8]{6,5,4,3,2,1,0:T(8,128)} %copy.25) | data formatting | bytes 2097152 | tf_op jit(solution)/shard_map/reshape | solution.py:112
  132.5 6.0 %multiply_reduce_fusion.1 = (f32[8]{0:T(128)}, f32[8]{0:T(128)}, f32[8,16,16,128]{3,2,1,0:T(8,128)S(1)}) fusion(f32[8,16,16,128]{3,2,1,0:T(8,128)S(1)} %reshape.119, f32[8,16,16,128]{3,2,1,0:T(8,128)S(1)} %copy-done.1, f32[16,16,128]{2,1,0:T(8,128)S(1)} %mul.300, f32[8,18,1,128]{3,2,1,0:T(1,128)} %copy-done.33, f32[8,18,16,128]{3,2,1,0:T(8,128)} %copy-done.7, ...), kind=kLoop, calls=%fused_computation.104 | loop fusion | flops 8912880 | bytes 5673280 | tf_op jit(solution)/shard_map/reduce_sum | solution.py:45
  138.5 30.7 %all-reduce.1 = (f32[8]{0:T(128)}, f32[8]{0:T(128)}) all-reduce(f32[8]{0:T(128)} %get-tuple-element.10, f32[8]{0:T(128)} %get-tuple-element.9), channel_id=1, replica_groups=mesh['span'=2,'height'=4,'depth'=4] {'height','depth'}, use_global_device_ids=true, to_apply=%region_3.4 | all-reduce | flops 16 | bytes 128 | tf_op jit(solution)/shard_map/psum | solution.py:50
  169.2 6.0 %all-reduce.3 = (f32[8]{0:T(128)}, f32[8]{0:T(128)}) all-reduce(f32[8]{0:T(128)} %get-tuple-element.13, f32[8]{0:T(128)} %get-tuple-element.14), channel_id=1, replica_groups=mesh['span'=2,'height'=4,'depth'=4] {'span'}, use_global_device_ids=true, to_apply=%region_4.5 | all-reduce | flops 16 | bytes 128 | tf_op jit(solution)/shard_map/psum | solution.py:49
  177.4 11.9 %reshape.121 = bf16[8,2,8,2,8,16,8]{6,5,4,3,2,1,0:T(8,128)(2,1)} reshape(bf16[8,16,16,128]{3,2,1,0:T(8,128)(2,1)} %fusion.87) | data formatting | bytes 1048576 | tf_op jit(solution)/shard_map/reshape | solution.py:98
  189.3 6.2 %bitcast_convert_fusion = bf16[16,8,8,8,8]{0,4,3,2,1:T(8,128)(2,1)S(1)} fusion(bf16[8,2,8,2,8,16,8]{6,5,4,3,2,1,0:T(8,128)(2,1)} %reshape.121, f32[2,2,16]{2,1,0:T(2,128)} %copy-done.41, s32[2,2,16]{2,1,0:T(2,128)} %copy-done.44), kind=kOutput, calls=%fused_computation.2 | convolution fusion | flops 8456192 | bytes 655872 | tf_op jit(solution)/shard_map/sxyz,lxiyjzk->slijk/dot_general | solution.py:101
  195.9 6.9 %all_to_all.20 = bf16[16,8,512]{2,1,0:T(8,128)(2,1)S(1)} all-to-all(bf16[16,8,512]{2,1,0:T(8,128)(2,1)S(1)} %copy.31), channel_id=1, replica_groups=mesh['span'=2,'height'=4,'depth'=4] {'span'}, dimensions={0} | all-to-all | bytes 262144 | tf_op jit(solution)/shard_map/all_to_all | solution.py:106
  202.8 5.6 %fusion.124 = f32[16,8,512]{2,1,0:T(8,128)S(1)} fusion(bf16[16,8,512]{2,1,0:T(8,128)(2,1)S(1)} %all_to_all.20, bf16[16,512,512]{2,1,0:T(8,128)(2,1)} %param.9), kind=kOutput, calls=%fused_computation.251 | convolution fusion | flops 67108864 | bytes 8781824 | tf_op jit(solution)/shard_map/sij,slj->sli/dot_general | solution.py:94
  208.4 7.7 %all_to_all.21 = f32[16,8,512]{2,1,0:T(8,128)S(1)} all-to-all(f32[16,8,512]{2,1,0:T(8,128)S(1)} %fusion.124), channel_id=1, replica_groups=mesh['span'=2,'height'=4,'depth'=4] {'span'}, dimensions={0} | all-to-all | bytes 524288 | tf_op jit(solution)/shard_map/all_to_all | solution.py:95
  218.1 10.1 %convolution_bitcast_fusion = f32[8,2,8,2,8,16,8]{5,6,3,1,4,2,0:T(8,128)} fusion(f32[16,8,8,8,8,1,1]{0,4,6,5,3,2,1:T(8,128)} %bitcast.147, f32[2,2,16]{2,1,0:T(2,128)S(1)} %copy-done.43, s32[2,2,16]{2,1,0:T(2,128)S(1)} %copy-done.45), kind=kOutput, calls=%fused_computation | convolution fusion | flops 50333696 | bytes 1311232 | tf_op jit(solution)/shard_map/sxyz,slijk->lxiyjzk/dot_general | solution.py:109
  228.1 12.3 %copy.33 = f32[8,2,8,2,8,16,8]{6,5,4,3,2,1,0:T(8,128)} copy(f32[8,2,8,2,8,16,8]{5,6,3,1,4,2,0:T(8,128)} %convolution_bitcast_fusion) | data formatting | bytes 2097152 | tf_op jit(solution)/shard_map/sxyz,slijk->lxiyjzk/transpose | solution.py:109
  240.4 11.9 %reshape.124 = f32[8,16,16,128]{3,2,1,0:T(8,128)S(1)} reshape(f32[8,2,8,2,8,16,8]{6,5,4,3,2,1,0:T(8,128)} %copy.33) | data formatting | bytes 2097152 | tf_op jit(solution)/shard_map/reshape | solution.py:112
  260.2 4.5 %collective-permute-start.12 = (f32[8,1,16,128]{3,2,1,0:T(8,128)S(1)}, f32[8,1,16,128]{3,2,1,0:T(8,128)S(1)}, u32[]{:S(2)}, u32[]{:S(2)}) collective-permute-start(f32[8,1,16,128]{3,2,1,0:T(8,128)S(1)} %get-tuple-element.38), channel_id=1, source_target_pairs={{16,0},{17,1},{18,2},{19,3},{20,4},{21,5},{22,6},{23,7},{24,8},{25... | collective-permute-start | bytes 196616 | tf_op jit(solution)/shard_map/ppermute | solution.py:24
  300.4 5.0 %fusion.22 = f32[8]{0:T(128)S(1)} fusion(f32[8,16,16,128]{3,2,1,0:T(8,128)S(1)} %reshape.124, f32[8,18,18,1]{3,2,1,0:T(8,128)} %copy.37, f32[8,18,1,128]{3,2,1,0:T(1,128)S(1)} %collective-permute-done.14, f32[8,18,16,128]{3,2,1,0:T(8,128)} %copy-done.8, f32[8,18,1,128]{3,2,1,0:T(1,128)} %copy-done.35, f32[8,18,18,1]{3,2,1,0:T(8,128)} %copy.35, ...), kind=kLoop, calls=%fused_computation.48 | loop fusion | flops 8126456 | bytes 3445024 | tf_op jit(solution)/shard_map/reduce_sum | solution.py:45
  305.5 30.6 %all-reduce = (f32[8]{0:T(128)S(1)}, f32[8]{0:T(128)S(1)}) all-reduce(f32[8]{0:T(128)S(1)} %copy-done.59, f32[8]{0:T(128)S(1)} %fusion.22), channel_id=1, replica_groups=mesh['span'=2,'height'=4,'depth'=4] {'height','depth'}, use_global_device_ids=true, to_apply=%region_9.10 | all-reduce | flops 16 | bytes 128 | tf_op jit(solution)/shard_map/psum | solution.py:50
  336.1 4.9 %all-reduce.2 = (f32[8]{0:T(128)S(1)}, f32[8]{0:T(128)S(1)}) all-reduce(f32[8]{0:T(128)S(1)} %get-tuple-element.11, f32[8]{0:T(128)S(1)} %get-tuple-element.12), channel_id=1, replica_groups=mesh['span'=2,'height'=4,'depth'=4] {'span'}, use_global_device_ids=true, to_apply=%region_10.11 | all-reduce | flops 16 | bytes 128 | tf_op jit(solution)/shard_map/psum | solution.py:49
  385.2 41.3 %pmax.7 = f32[]{:T(128)} all-reduce(f32[]{:T(128)} %get-tuple-element.19), channel_id=1, replica_groups=mesh['span'=2,'height'=4,'depth'=4] {'span','height','depth'}, use_global_device_ids=true, to_apply=%region_21.22 | all-reduce | flops 1 | bytes 8 | tf_op jit(solution)/shard_map/pmax | solution.py:144
  (271 shorter events, 181.6 us)
Async XLA Ops:
  5.8 15.1 %collective-permute-start = (f32[2,1,16,128]{3,2,1,0:T(8,128)S(1)}, f32[2,1,16,128]{3,2,1,0:T(8,128)S(1)}, u32[]{:S(2)}, u32[]{:S(2)}) collective-permute-start(f32[2,1,16,128]{3,2,1,0:T(8,128)S(1)} %get-tuple-element.53), channel_id=1, source_target_pairs={{16,0},{17,1},{18,2},{19,3},{20,4},{21,5},{22,6},{23,7},{24,8},{25... | collective-permute-start | bytes 49160 | tf_op jit(solution)/shard_map/ppermute | solution.py:24
  8.2 12.6 %collective-permute-start.2 = (f32[2,1,16,128]{3,2,1,0:T(8,128)S(1)}, f32[2,1,16,128]{3,2,1,0:T(8,128)S(1)}, u32[]{:S(2)}, u32[]{:S(2)}) collective-permute-start(f32[2,1,16,128]{3,2,1,0:T(8,128)S(1)} %get-tuple-element.52), channel_id=1, source_target_pairs={{0,16},{1,17},{2,18},{3,19},{4,20},{5,21},{6,22},{7,23},{8,24},{9,... | collective-permute-start | bytes 49160 | tf_op jit(solution)/shard_map/ppermute | solution.py:21
  20.9 17.6 %collective-permute-start.4 = (f32[2,18,1,128]{3,2,1,0:T(1,128)S(1)}, f32[2,18,1,128]{3,2,1,0:T(1,128)S(1)}, u32[]{:S(2)}, u32[]{:S(2)}) collective-permute-start(f32[2,18,1,128]{3,2,1,0:T(1,128)S(1)} %get-tuple-element.51), channel_id=1, source_target_pairs={{4,0},{8,4},{12,8},{5,1},{9,5},{13,9},{6,2},{10,6},{14,10},{7,3},{... | collective-permute-start | bytes 55304 | tf_op jit(solution)/shard_map/ppermute | solution.py:24
  22.8 15.7 %collective-permute-start.6 = (f32[2,18,1,128]{3,2,1,0:T(1,128)S(1)}, f32[2,18,1,128]{3,2,1,0:T(1,128)S(1)}, u32[]{:S(2)}, u32[]{:S(2)}) collective-permute-start(f32[2,18,1,128]{3,2,1,0:T(1,128)S(1)} %get-tuple-element.50), channel_id=1, source_target_pairs={{0,4},{4,8},{8,12},{1,5},{5,9},{9,13},{2,6},{6,10},{10,14},{3,7},{... | collective-permute-start | bytes 55304 | tf_op jit(solution)/shard_map/ppermute | solution.py:21
  32.5 13.9 %all-to-all-start = ((bf16[16,8,512]{2,1,0:T(8,128)(2,1)}), bf16[16,8,512]{2,1,0:T(8,128)(2,1)S(1)}, u32[]{:S(2)}, u32[]{:S(2)}) async-start(bf16[16,8,512]{2,1,0:T(8,128)(2,1)} %copy.23), calls=%async_computation | async-start | bytes 262144 | tf_op jit(solution)/shard_map/all_to_all | solution.py:106
  39.6 69.7 %collective-permute-start.10 = (f32[2,18,18,1]{3,2,1,0:T(8,128)}, f32[2,18,18,1]{3,2,1,0:T(8,128)}, u32[]{:S(2)}, u32[]{:S(2)}) collective-permute-start(f32[2,18,18,1]{3,2,1,0:T(8,128)} %get-tuple-element.49), channel_id=1, source_target_pairs={{0,1},{1,2},{2,3},{4,5},{5,6},{6,7},{8,9},{9,10},{10,11},{12,13},{... | collective-permute-start | bytes 7784 | tf_op jit(solution)/shard_map/ppermute | solution.py:21
  43.1 83.0 %collective-permute-start.8 = (f32[2,18,18,1]{3,2,1,0:T(8,128)}, f32[2,18,18,1]{3,2,1,0:T(8,128)}, u32[]{:S(2)}, u32[]{:S(2)}) collective-permute-start(f32[2,18,18,1]{3,2,1,0:T(8,128)} %get-tuple-element.48), channel_id=1, source_target_pairs={{1,0},{2,1},{3,2},{5,4},{6,5},{7,6},{9,8},{10,9},{11,10},{13,12},{... | collective-permute-start | bytes 7784 | tf_op jit(solution)/shard_map/ppermute | solution.py:24
  52.7 7.9 %all-to-all-start.1 = ((f32[16,8,512]{2,1,0:T(8,128)}), f32[16,8,512]{2,1,0:T(8,128)}, u32[]{:S(2)}, u32[]{:S(2)}) async-start(f32[16,8,512]{2,1,0:T(8,128)} %fusion.123), calls=%async_computation.1 | async-start | bytes 524288 | tf_op jit(solution)/shard_map/all_to_all | solution.py:95
  117.9 10.2 %collective-permute-start.11 = (f32[8,18,18,1]{2,0,3,1:T(8,128)S(1)}, f32[8,18,18,1]{2,0,3,1:T(8,128)S(1)}, u32[]{:S(2)}, u32[]{:S(2)}) collective-permute-start(f32[8,18,18,1]{2,0,3,1:T(8,128)S(1)} %copy.28), channel_id=1, source_target_pairs={{0,1},{1,2},{2,3},{4,5},{5,6},{6,7},{8,9},{9,10},{10,11},{12,13},{... | collective-permute-start | bytes 31112 | tf_op jit(solution)/shard_map/ppermute | solution.py:21
  123.0 7.3 %collective-permute-start.9 = (f32[8,18,18,1]{2,0,3,1:T(8,128)S(1)}, f32[8,18,18,1]{2,0,3,1:T(8,128)S(1)}, u32[]{:S(2)}, u32[]{:S(2)}) collective-permute-start(f32[8,18,18,1]{2,0,3,1:T(8,128)S(1)} %copy.26), channel_id=1, source_target_pairs={{1,0},{2,1},{3,2},{5,4},{6,5},{7,6},{9,8},{10,9},{11,10},{13,12},{... | collective-permute-start | bytes 31112 | tf_op jit(solution)/shard_map/ppermute | solution.py:24
  252.3 12.4 %collective-permute-start.13 = (f32[8,1,16,128]{3,2,1,0:T(8,128)S(1)}, f32[8,1,16,128]{3,2,1,0:T(8,128)S(1)}, u32[]{:S(2)}, u32[]{:S(2)}) collective-permute-start(f32[8,1,16,128]{3,2,1,0:T(8,128)S(1)} %get-tuple-element.39), channel_id=1, source_target_pairs={{0,16},{1,17},{2,18},{3,19},{4,20},{5,21},{6,22},{7,23},{8,24},{9,... | collective-permute-start | bytes 196616 | tf_op jit(solution)/shard_map/ppermute | solution.py:21
  254.3 17.7 %collective-permute-start.25 = (bf16[1,16,128]{2,1,0:T(8,128)(2,1)S(1)}, bf16[1,16,128]{2,1,0:T(8,128)(2,1)S(1)}, u32[]{:S(2)}, u32[]{:S(2)}) collective-permute-start(bf16[1,16,128]{2,1,0:T(8,128)(2,1)S(1)} %get-tuple-element.67), channel_id=1, source_target_pairs={{16,0},{17,1},{18,2},{19,3},{20,4},{21,5},{22,6},{23,7},{24,8},{25... | collective-permute-start | bytes 12296 | tf_op jit(solution)/shard_map/ppermute | solution.py:24
  258.9 13.2 %collective-permute-start.24 = (bf16[1,16,128]{2,1,0:T(8,128)(2,1)S(1)}, bf16[1,16,128]{2,1,0:T(8,128)(2,1)S(1)}, u32[]{:S(2)}, u32[]{:S(2)}) collective-permute-start(bf16[1,16,128]{2,1,0:T(8,128)(2,1)S(1)} %get-tuple-element.66), channel_id=1, source_target_pairs={{0,16},{1,17},{2,18},{3,19},{4,20},{5,21},{6,22},{7,23},{8,24},{9,... | collective-permute-start | bytes 12296 | tf_op jit(solution)/shard_map/ppermute | solution.py:21
  260.2 7.4 %collective-permute-start.12 = (f32[8,1,16,128]{3,2,1,0:T(8,128)S(1)}, f32[8,1,16,128]{3,2,1,0:T(8,128)S(1)}, u32[]{:S(2)}, u32[]{:S(2)}) collective-permute-start(f32[8,1,16,128]{3,2,1,0:T(8,128)S(1)} %get-tuple-element.38), channel_id=1, source_target_pairs={{16,0},{17,1},{18,2},{19,3},{20,4},{21,5},{22,6},{23,7},{24,8},{25... | collective-permute-start | bytes 196616 | tf_op jit(solution)/shard_map/ppermute | solution.py:24
  267.7 9.7 %collective-permute-start.14 = (f32[8,18,1,128]{3,2,1,0:T(1,128)S(1)}, f32[8,18,1,128]{3,2,1,0:T(1,128)S(1)}, u32[]{:S(2)}, u32[]{:S(2)}) collective-permute-start(f32[8,18,1,128]{3,2,1,0:T(1,128)S(1)} %get-tuple-element.33), channel_id=1, source_target_pairs={{4,0},{8,4},{12,8},{5,1},{9,5},{13,9},{6,2},{10,6},{14,10},{7,3},{... | collective-permute-start | bytes 221192 | tf_op jit(solution)/shard_map/ppermute | solution.py:24
  269.6 7.8 %collective-permute-start.15 = (f32[8,18,1,128]{3,2,1,0:T(1,128)S(1)}, f32[8,18,1,128]{3,2,1,0:T(1,128)S(1)}, u32[]{:S(2)}, u32[]{:S(2)}) collective-permute-start(f32[8,18,1,128]{3,2,1,0:T(1,128)S(1)} %get-tuple-element.32), channel_id=1, source_target_pairs={{0,4},{4,8},{8,12},{1,5},{5,9},{9,13},{2,6},{6,10},{10,14},{3,7},{... | collective-permute-start | bytes 221192 | tf_op jit(solution)/shard_map/ppermute | solution.py:21
  272.1 21.2 %collective-permute-start.27 = (bf16[18,1,128]{2,1,0:T(2,128)(2,1)S(1)}, bf16[18,1,128]{2,1,0:T(2,128)(2,1)S(1)}, u32[]{:S(2)}, u32[]{:S(2)}) collective-permute-start(bf16[18,1,128]{2,1,0:T(2,128)(2,1)S(1)} %get-tuple-element.63), channel_id=1, source_target_pairs={{4,0},{8,4},{12,8},{5,1},{9,5},{13,9},{6,2},{10,6},{14,10},{7,3},{... | collective-permute-start | bytes 13832 | tf_op jit(solution)/shard_map/ppermute | solution.py:24
  275.3 18.0 %collective-permute-start.26 = (bf16[18,1,128]{2,1,0:T(2,128)(2,1)S(1)}, bf16[18,1,128]{2,1,0:T(2,128)(2,1)S(1)}, u32[]{:S(2)}, u32[]{:S(2)}) collective-permute-start(bf16[18,1,128]{2,1,0:T(2,128)(2,1)S(1)} %get-tuple-element.62), channel_id=1, source_target_pairs={{0,4},{4,8},{8,12},{1,5},{5,9},{9,13},{2,6},{6,10},{10,14},{3,7},{... | collective-permute-start | bytes 13832 | tf_op jit(solution)/shard_map/ppermute | solution.py:21
  283.8 10.3 %collective-permute-start.17 = (f32[8,18,18,1]{2,0,3,1:T(8,128)}, f32[8,18,18,1]{2,0,3,1:T(8,128)}, u32[]{:S(2)}, u32[]{:S(2)}) collective-permute-start(f32[8,18,18,1]{2,0,3,1:T(8,128)} %copy.36), channel_id=1, source_target_pairs={{0,1},{1,2},{2,3},{4,5},{5,6},{6,7},{8,9},{9,10},{10,11},{12,13},{... | collective-permute-start | bytes 31112 | tf_op jit(solution)/shard_map/ppermute | solution.py:21
  289.2 8.0 %collective-permute-start.16 = (f32[8,18,18,1]{2,0,3,1:T(8,128)}, f32[8,18,18,1]{2,0,3,1:T(8,128)}, u32[]{:S(2)}, u32[]{:S(2)}) collective-permute-start(f32[8,18,18,1]{2,0,3,1:T(8,128)} %copy.34), channel_id=1, source_target_pairs={{1,0},{2,1},{3,2},{5,4},{6,5},{7,6},{9,8},{10,9},{11,10},{13,12},{... | collective-permute-start | bytes 31112 | tf_op jit(solution)/shard_map/ppermute | solution.py:24
  342.0 11.7 %collective-permute-start.18 = (f32[8,1,16,128]{3,2,1,0:T(8,128)S(1)}, f32[8,1,16,128]{3,2,1,0:T(8,128)S(1)}, u32[]{:S(2)}, u32[]{:S(2)}) collective-permute-start(f32[8,1,16,128]{3,2,1,0:T(8,128)S(1)} %get-tuple-element.37), channel_id=1, source_target_pairs={{16,0},{17,1},{18,2},{19,3},{20,4},{21,5},{22,6},{23,7},{24,8},{25... | collective-permute-start | bytes 196616 | tf_op jit(solution)/shard_map/ppermute | solution.py:24
  345.4 8.2 %collective-permute-start.19 = (f32[8,1,16,128]{3,2,1,0:T(8,128)S(1)}, f32[8,1,16,128]{3,2,1,0:T(8,128)S(1)}, u32[]{:S(2)}, u32[]{:S(2)}) collective-permute-start(f32[8,1,16,128]{3,2,1,0:T(8,128)S(1)} %get-tuple-element.36), channel_id=1, source_target_pairs={{0,16},{1,17},{2,18},{3,19},{4,20},{5,21},{6,22},{7,23},{8,24},{9,... | collective-permute-start | bytes 196616 | tf_op jit(solution)/shard_map/ppermute | solution.py:21
  347.8 10.3 %collective-permute-start.29 = (bf16[18,18,1]{2,1,0:T(8,128)(2,1)S(1)}, bf16[18,18,1]{2,1,0:T(8,128)(2,1)S(1)}, u32[]{:S(2)}, u32[]{:S(2)}) collective-permute-start(bf16[18,18,1]{2,1,0:T(8,128)(2,1)S(1)} %get-tuple-element.59), channel_id=1, source_target_pairs={{1,0},{2,1},{3,2},{5,4},{6,5},{7,6},{9,8},{10,9},{11,10},{13,12},{... | collective-permute-start | bytes 1952 | tf_op jit(solution)/shard_map/ppermute | solution.py:24
  366.5 8.4 %collective-permute-start.22 = (f32[8,18,18,1]{2,0,3,1:T(8,128)}, f32[8,18,18,1]{2,0,3,1:T(8,128)}, u32[]{:S(2)}, u32[]{:S(2)}) collective-permute-start(f32[8,18,18,1]{2,0,3,1:T(8,128)} %copy.38), channel_id=1, source_target_pairs={{1,0},{2,1},{3,2},{5,4},{6,5},{7,6},{9,8},{10,9},{11,10},{13,12},{... | collective-permute-start | bytes 31112 | tf_op jit(solution)/shard_map/ppermute | solution.py:24
  (76 other events, 863.8 us)
